TPU v7x, 32 devices: a whole 2x2x4 slice. The times are simulated.
32 devices in a mesh: seq: 2 (over x), ctx: 4 (over y, core), exp: 4 (over z).
Axes of the slice: x: 2, y: 2, z: 4, core: 2. Of those that a mesh axis runs over, the one named last changes fastest.
Arguments:
- tokens: bfloat16 [2, 2048, 7168], P('seq', ('ctx', 'exp')), may hold values from -8 to 8
- routing: int32 [2, 2048, 8], P('seq', ('ctx', 'exp')), may hold values from 0 to 255, as said below
- router_weight: bfloat16 [7168, 256], replicated, may hold values from -0.0625 to 0.0625
- w_gate: bfloat16 [8, 7168, 2048], P(('seq', 'exp'), None, 'ctx'), may hold values from -0.0625 to 0.0625
- w_up: bfloat16 [8, 7168, 2048], P(('seq', 'exp'), None, 'ctx'), may hold values from -0.0625 to 0.0625
- w_down: bfloat16 [8, 2048, 7168], P(('seq', 'exp'), 'ctx'), may hold values from -0.125 to 0.125
Outputs:
- routed: bfloat16 [2, 2048, 7168], P('seq', ('ctx', 'exp'))
- balance: float32 [2, 256], P('seq')
Inputs may be any that keep to these rules, and one draw needn't show every extreme that they name: `routing`: each token names 8 different experts. The rows of one device name any one expert at least 3 and at most 5 times; in every draw one expert below 8 is named exactly 5 times by the rows of every device.
All inputs are finite; a program needn't handle non-finite values.
Results may differ from a plain program's by a relative error of at most 0.014.
Values may be sent and summed in bfloat16 or wider, within the bound.
A program may use at most 128 MiB of HBM per device.

v0:
```python
import jax
import jax.numpy as jnp
from jax import lax
from jax.sharding import PartitionSpec as P

route_scale = 2.5


def project_rows(row_block, weight):
    layout = row_block.shape
    product = jnp.dot(row_block.reshape(-1, layout[-1]), weight, preferred_element_type=jnp.float32)
    return product.reshape(layout[:-1] + (weight.shape[1],))


def on_device(tokens, routing, router_weight, w_gate, w_up, w_down):
    token_rows = tokens[0]
    routes = routing[0]
    token_count, feature_count = token_rows.shape
    top_count = routes.shape[1]
    experts = router_weight.shape[1]
    seq_count = lax.axis_size("seq")
    ctx_count = lax.axis_size("ctx")
    exp_count = lax.axis_size("exp")
    flight = seq_count * exp_count
    mean_load = token_count * top_count // experts
    capacity = mean_load + mean_load // 4
    length = token_count * ctx_count * exp_count
    logits = jnp.dot(token_rows, router_weight, preferred_element_type=jnp.float32)
    scores = jax.nn.sigmoid(logits)
    affinity = scores / jnp.sum(scores, axis=1, keepdims=True)
    picked = jnp.take_along_axis(scores, routes, axis=1)
    gate_weights = picked / jnp.sum(picked, axis=1, keepdims=True) * route_scale
    expert_iota = lax.broadcasted_iota(jnp.int32, (1, 1, experts), 2)
    load_part = jnp.sum((routes[:, :, None] == expert_iota).astype(jnp.float32), axis=(0, 1))
    prob_part = jnp.sum(affinity, axis=0)
    prob_sum, load_sum = lax.psum((prob_part, load_part), ("ctx", "exp"))
    balance = load_sum * (experts / (top_count * length)) * (prob_sum / length) * experts
    assignments = routes.reshape(-1)
    flight_iota = lax.broadcasted_iota(jnp.int32, (1, flight), 1)
    onehot = (assignments[:, None] == flight_iota).astype(jnp.int32)
    slot_rank = jnp.sum((jnp.cumsum(onehot, axis=0) - onehot) * onehot, axis=1)
    is_live = assignments < flight
    slot_index = jnp.where(is_live, assignments * capacity + slot_rank, flight * capacity)
    slot_iota = lax.broadcasted_iota(jnp.int32, (1, flight * capacity), 1)
    matches = slot_index[:, None] == slot_iota
    owner_iota = lax.broadcasted_iota(jnp.int32, (assignments.shape[0], 1), 0) // top_count
    source_row = jnp.sum(jnp.where(matches, owner_iota, 0), axis=0)
    filled = jnp.any(matches, axis=0)
    outgoing = jnp.where(filled[:, None], token_rows[source_row], jnp.zeros((), jnp.bfloat16))
    outgoing = outgoing.reshape(flight, capacity, feature_count)
    row_block = lax.all_gather(
        lax.all_to_all(outgoing, ("seq", "exp"), split_axis=0, concat_axis=0, tiled=True),
        "ctx",
        axis=0,
        tiled=True,
    )
    gate_proj = project_rows(row_block, w_gate[0])
    up_proj = project_rows(row_block, w_up[0])
    hidden = (jax.nn.silu(gate_proj) * up_proj).astype(jnp.bfloat16)
    summed = lax.psum_scatter(
        project_rows(hidden, w_down[0]).astype(jnp.bfloat16), "ctx", scatter_dimension=0, tiled=True
    )
    returned = lax.all_to_all(summed, ("seq", "exp"), split_axis=0, concat_axis=0, tiled=True)
    returned = returned.reshape(flight * capacity, feature_count)
    live_gates = jnp.where(is_live.reshape(token_count, top_count), gate_weights, 0.0)
    row_index = jnp.where(is_live, slot_index, 0).reshape(token_count, top_count)
    combined = jnp.zeros((token_count, feature_count), jnp.float32)
    for column in range(top_count):
        combined = combined + live_gates[:, column : column + 1] * returned[row_index[:, column]]
    return (combined.astype(jnp.bfloat16)[None], balance[None])


def solution(mesh):
    placed = (
        P("seq", ("ctx", "exp"), None),
        P("seq", ("ctx", "exp"), None),
        P(),
        P(("seq", "exp"), None, "ctx"),
        P(("seq", "exp"), None, "ctx"),
        P(("seq", "exp"), "ctx", None),
    )
    return jax.shard_map(
        on_device,
        mesh=mesh,
        in_specs=placed,
        out_specs=(P("seq", ("ctx", "exp"), None), P("seq", None)),
        check_vma=False,
    )
```

profile of v0, /device:TPU:0, one launch (start us, length us, event | category | flops | bytes accessed | tf_op | source)
XLA Modules:
  0.0 198.0 jit_solution(13050393516363820651)
XLA Ops:
  7.2 0.9 copy.30
  8.3 2.3 %reduce-window.6 = s32[8,8,128]{2,1,0:T(8,128)S(1)} reduce-window(s32[8,8,128]{2,1,0:T(8,128)S(1)} %fusion.35, s32[]{:T(128)} %constant.22.clone.1), window={size=1x1x128 pad=0_0x0_0x127_0}, to_apply=%region_1.0 | reduce-window | flops 1040384 | bytes 65540 | tf_op jit(solution)/shard_map/reduce-window
  11.6 0.9 gather_fusion
  12.9 30.9 %all_to_all.10 = bf16[8,5,7168]{2,1,0:T(8,128)(2,1)S(1)} all-to-all(bf16[8,5,7168]{2,1,0:T(8,128)(2,1)S(1)} %broadcast_select_fusion), channel_id=1, replica_groups=mesh['seq'=2,'ctx'=4,'exp'=4] {'seq','exp'}, dimensions={0} | all-to-all | bytes 1146880 | tf_op jit(solution)/shard_map/all_to_all | solution.py:52
  43.8 1.2 copy.34
  45.0 21.4 %all-gather.2.cloned.1.call-done = bf16[32,5,7168]{2,0,1:T(8,128)(2,1)} async-done(((bf16[8,5,7168]{2,0,1:T(8,128)(2,1)}), bf16[32,5,7168]{2,0,1:T(8,128)(2,1)}) %all-gather.2.cloned.1.call-update) | async-done | bytes 2293776 | tf_op jit(solution)/shard_map/all_gather | solution.py:51
  66.4 5.1 %fusion.4 = f32[32,5,512]{2,0,1:T(8,128)S(1)} fusion(bf16[32,5,7168]{2,0,1:T(8,128)(2,1)} %all-gather.2.cloned.1.call-done, bf16[1,7168,512]{2,1,0:T(8,128)(2,1)} %param.9), kind=kOutput, calls=%fused_computation.15 | convolution fusion | flops 1174405120 | bytes 9961472 | tf_op jit(solution)/shard_map/dot_general | solution.py:11
  71.6 9.9 %fusion = bf16[5,4,8,7168]{3,2,1,0:T(8,128)(2,1)} fusion(bf16[1,512,7168]{2,1,0:T(8,128)(2,1)} %param.11, bf16[32,5,7168]{2,0,1:T(8,128)(2,1)} %all-gather.2.cloned.1.call-done, bf16[1,7168,512]{2,1,0:T(8,128)(2,1)} %param.10, f32[32,5,512]{2,0,1:T(8,128)S(1)} %fusion.4), kind=kOutput, calls=%fused_computation.11 | convolution fusion | flops 2350448640 | bytes 19595264 | tf_op jit(solution)/shard_map/dot_general | solution.py:11
  81.5 3.1 %copy.38 = bf16[5,4,8,7168]{3,2,0,1:T(8,128)(2,1)} copy(bf16[5,4,8,7168]{3,2,1,0:T(8,128)(2,1)} %fusion) | data formatting | bytes 4587520
  85.5 2.8 %fusion.45 = (f32[128]{0:T(128)S(1)}, f32[128,256]{1,0:T(8,128)S(1)}, f32[128,256]{1,0:T(8,128)S(1)}) fusion(bf16[7168,256]{1,0:T(8,128)(2,1)} %param.8, bf16[1,128,7168]{2,1,0:T(8,128)(2,1)S(1)} %copy-done), kind=kOutput, calls=%fused_computation.111 | convolution fusion | flops 469892992 | bytes 5767680 | tf_op jit(solution)/shard_map/dot_general | solution.py:28
  88.3 8.6 %gather_fusion.9 = f32[1024]{0:T(1024)S(1)} fusion(f32[128,256]{1,0:T(8,128)S(1)} %get-tuple-element.21, s32[1024]{0:T(1024)S(1)} %reshape.577), kind=kCustom, calls=%fused_computation.9 | custom fusion | bytes 16384 | tf_op jit(solution)/shard_map/jit(take_along_axis)/gather | solution.py:31
  97.3 33.1 %all-reduce = (f32[256]{0:T(256)S(1)}, f32[256]{0:T(256)S(1)}) all-reduce(f32[256]{0:T(256)S(1)} %fusion.23, f32[256]{0:T(256)S(1)} %convert_reduce_fusion), channel_id=1, replica_groups=mesh['seq'=2,'ctx'=4,'exp'=4] {'ctx','exp'}, use_global_device_ids=true, to_apply=%region_11.12 | all-reduce | flops 512 | bytes 4096 | tf_op jit(solution)/shard_map/psum | solution.py:36
  130.8 2.3 %copy.35 = bf16[8,5,7168]{2,1,0:T(8,128)(2,1)} copy(bf16[8,5,7168]{2,0,1:T(8,128)(2,1)} %bitcast.97) | data formatting | bytes 1146880 | tf_op jit(solution)/shard_map/reduce_scatter | solution.py:60
  133.2 3.7 %all-to-all-start.1 = ((bf16[8,5,7168]{2,1,0:T(8,128)(2,1)}), bf16[8,5,7168]{2,1,0:T(8,128)(2,1)S(1)}, u32[]{:S(2)}, u32[]{:S(2)}) async-start(bf16[8,5,7168]{2,1,0:T(8,128)(2,1)} %copy.35), calls=%async_computation.1 | async-start | bytes 1835008 | tf_op jit(solution)/shard_map/all_to_all | solution.py:63
  138.1 21.1 %all-to-all-done.1 = bf16[8,5,7168]{2,1,0:T(8,128)(2,1)S(1)} async-done(((bf16[8,5,7168]{2,1,0:T(8,128)(2,1)}), bf16[8,5,7168]{2,1,0:T(8,128)(2,1)S(1)}, u32[]{:S(2)}, u32[]{:S(2)}) %all-to-all-start.1) | async-done | bytes 573472 | tf_op jit(solution)/shard_map/all_to_all | solution.py:63
  159.5 2.9 %gather_fusion.8 = bf16[128,7168]{1,0:T(8,128)(2,1)} fusion(bf16[40,7168]{1,0:T(8,128)(2,1)S(1)} %reshape.496, s32[1024]{0:T(1024)S(1)} %get-tuple-element.23), kind=kCustom, calls=%fused_computation.8 | custom fusion | bytes 3670528 | tf_op jit(solution)/shard_map/gather | solution.py:69
  162.4 3.0 %gather_fusion.7 = bf16[128,7168]{1,0:T(8,128)(2,1)} fusion(bf16[40,7168]{1,0:T(8,128)(2,1)S(1)} %reshape.496, s32[1024]{0:T(1024)S(1)} %get-tuple-element.24), kind=kCustom, calls=%fused_computation.7 | custom fusion | bytes 3670528 | tf_op jit(solution)/shard_map/gather | solution.py:69
  165.4 2.9 %gather_fusion.6 = bf16[128,7168]{1,0:T(8,128)(2,1)} fusion(bf16[40,7168]{1,0:T(8,128)(2,1)S(1)} %reshape.496, s32[1024]{0:T(1024)S(1)} %get-tuple-element.25), kind=kCustom, calls=%fused_computation.6 | custom fusion | bytes 3670528 | tf_op jit(solution)/shard_map/gather | solution.py:69
  168.3 3.0 %gather_fusion.5 = bf16[128,7168]{1,0:T(8,128)(2,1)} fusion(bf16[40,7168]{1,0:T(8,128)(2,1)S(1)} %reshape.496, s32[1024]{0:T(1024)S(1)} %get-tuple-element.26), kind=kCustom, calls=%fused_computation.5 | custom fusion | bytes 3670528 | tf_op jit(solution)/shard_map/gather | solution.py:69
  171.2 3.0 %gather_fusion.4 = bf16[128,7168]{1,0:T(8,128)(2,1)} fusion(bf16[40,7168]{1,0:T(8,128)(2,1)S(1)} %reshape.496, s32[1024]{0:T(1024)S(1)} %get-tuple-element.27), kind=kCustom, calls=%fused_computation.4 | custom fusion | bytes 3670528 | tf_op jit(solution)/shard_map/gather | solution.py:69
  174.2 3.0 %gather_fusion.3 = bf16[128,7168]{1,0:T(8,128)(2,1)} fusion(bf16[40,7168]{1,0:T(8,128)(2,1)S(1)} %reshape.496, s32[1024]{0:T(1024)S(1)} %get-tuple-element.28), kind=kCustom, calls=%fused_computation.3 | custom fusion | bytes 3670528 | tf_op jit(solution)/shard_map/gather | solution.py:69
  177.3 3.0 %gather_fusion.2 = bf16[128,7168]{1,0:T(8,128)(2,1)} fusion(bf16[40,7168]{1,0:T(8,128)(2,1)S(1)} %reshape.496, s32[1024]{0:T(1024)S(1)} %get-tuple-element.29), kind=kCustom, calls=%fused_computation.2 | custom fusion | bytes 3670528 | tf_op jit(solution)/shard_map/gather | solution.py:69
  180.2 2.9 %gather_fusion.1 = bf16[128,7168]{1,0:T(8,128)(2,1)} fusion(bf16[40,7168]{1,0:T(8,128)(2,1)S(1)} %reshape.496, s32[1024]{0:T(1024)S(1)} %get-tuple-element.30), kind=kCustom, calls=%fused_computation.1 | custom fusion | bytes 3670528 | tf_op jit(solution)/shard_map/gather | solution.py:69
  183.2 8.0 %fusion.7 = bf16[1,128,7168]{2,1,0:T(8,128)(2,1)} fusion(bf16[128,7168]{1,0:T(8,128)(2,1)} %gather_fusion.8, bf16[128,7168]{1,0:T(8,128)(2,1)} %gather_fusion.7, bf16[128,7168]{1,0:T(8,128)(2,1)} %gather_fusion.6, bf16[128,7168]{1,0:T(8,128)(2,1)} %gather_fusion.5, bf16[128,7168]{1,0:T(8,128)(2,1)} %gather_fusion.4, bf16[128,7168]{1,0:T(8,128)(2,1)} %gather_fusion.3, ...), kind=kLoop, calls=%fused_computation.19 | loop fusion | flops 22020096 | bytes 16519168 | tf_op jit(solution)/shard_map/convert_element_type | solution.py:70
  (43 shorter events, 4.7 us)
Async XLA Ops:
  7.2 4.4 %copy-start = (bf16[1,128,7168]{2,1,0:T(8,128)(2,1)S(1)}, bf16[1,128,7168]{2,1,0:T(8,128)(2,1)}, u32[]{:S(2)}) copy-start(bf16[1,128,7168]{2,1,0:T(8,128)(2,1)} %param.6) | copy-start | bytes 5505028
  7.2 59.3 %all-gather.2.cloned.1.call-start = ((), (), s32[]{:S(2)}) async-start(), calls=%async_computation.3 | async-start | bytes 2867200 | tf_op jit(solution)/shard_map/all_gather | solution.py:51
  45.0 85.8 %reduce-scatter.4.cloned.1.call-start = ((), (), s32[]{:S(2)}) async-start(), calls=%async_computation.4 | async-start | bytes 2867200
  84.6 0.7 copy-start.1
  133.2 26.0 %all-to-all-start.1 = ((bf16[8,5,7168]{2,1,0:T(8,128)(2,1)}), bf16[8,5,7168]{2,1,0:T(8,128)(2,1)S(1)}, u32[]{:S(2)}, u32[]{:S(2)}) async-start(bf16[8,5,7168]{2,1,0:T(8,128)(2,1)} %copy.35), calls=%async_computation.1 | async-start | bytes 1835008 | tf_op jit(solution)/shard_map/all_to_all | solution.py:63
Sparse Core Ops, SparseCore 0:
  45.1 21.2 all-gather.1
  84.8 32.5 reduce-scatter.3
where the time goes:
time: 198 us
  blocking collectives  64 us (32%)
  local copies, waits for them, and re-layouts  43.1 us (22%)
  waiting for transfers between devices  42.5 us (21%)
  matrix products  17.8 us (9%)
  between operations  14.2 us (7%)
  other arithmetic  12.5 us (6%)
  starting transfers between devices  3.81 us (2%)
    psum x1, blocking collectives, on_device(): prob_sum, load_sum = lax.psum((prob_part, load_part), ('ctx', 'exp'))  33.1 us
    all_to_all x1, blocking collectives, on_device(): lax.all_to_all(outgoing, ('seq', 'exp'), split_axis=0, concat_axis=0, til...  30.9 us
    gather x8, local copies, waits for them, and re-layouts, on_device(): returned[row_index[:, column]]  23.7 us
    all_gather x1, waiting for transfers between devices, on_device(): lax.all_gather(lax.all_to_all(outgoing, ('seq', 'exp'), split_axis=0, con...  21.4 us
    all_to_all x1, waiting for transfers between devices, on_device(): lax.all_to_all(summed, ('seq', 'exp'), split_axis=0, concat_axis=0, tiled...  21.1 us
    dot_general x2, matrix products, project_rows(): jnp.dot(row_block.reshape(-1, layout[-1]), weight, preferred_element_type...  15 us
    gather x4, local copies, waits for them, and re-layouts, on_device(): picked = jnp.take_along_axis(scores, routes, axis=1)  8.86 us
    convert_element_type x1, other arithmetic, on_device(): return (combined.astype(jnp.bfloat16)[None], balance[None])  7.96 us
  transfers between devices with their start and end apart: 3, of which 2 were waited for; matrix products, arithmetic and copies ran while one was open for 7% of the time, Pallas kernels for 0%

commit v1 on v0

v1 whole, which is shorter than its diff:
```python
import functools

import jax
import jax.numpy as jnp
from jax import lax
from jax.experimental import pallas as pl
from jax.experimental.pallas import tpu as pltpu
from jax.sharding import PartitionSpec as P

route_scale = 2.5
LANES = 128
SUBS = 8
MESH = pl.DeviceIdType.MESH
f32 = jnp.float32
bf16 = jnp.bfloat16


def dot(a, b):
    return jnp.dot(a, b, preferred_element_type=f32)


def pack(rows, cap):
    sub = lax.broadcasted_iota(jnp.int32, (1, SUBS, LANES), 1)
    pieces = []
    for q in range(cap):
        piece = rows[:, :, q * LANES : (q + 1) * LANES]
        for s in range(cap, SUBS):
            piece = jnp.where(sub == s, rows[:, q : q + 1, s * LANES : (s + 1) * LANES], piece)
        pieces.append(piece)
    return jnp.concatenate(pieces, axis=2)


def unpack(dense, cap):
    sub = lax.broadcasted_iota(jnp.int32, (1, SUBS, LANES), 1)
    pieces = []
    for b in range(SUBS):
        if b < cap:
            piece = dense[:, :, b * LANES : (b + 1) * LANES]
        else:
            piece = jnp.broadcast_to(dense[:, b : b + 1, 0:LANES], dense.shape[:2] + (LANES,))
            for r in range(1, cap):
                piece = jnp.where(sub == r, dense[:, b : b + 1, r * LANES : (r + 1) * LANES], piece)
        pieces.append(piece)
    return jnp.concatenate(pieces, axis=2)


def kernel(
    cfg,
    tokens, routes, routes_t, router_weight, w_gate, w_up, w_down,
    out, bal,
    tok, rw, wg, wu, wd, outv,
    mout, minn, xs, acc, sel_s, gates, hid,
    ps, pr, keep, ys, yr, ykeep, rout, rin, stat,
    tok_sem, rw_sem, wg_sem, wu_sem, wd_sem, out_sem,
    d_send, d_recv, y_send, y_recv, c_send, c_recv,
    p_send, p_recv, v_send, v_recv, r_send, r_recv, s_send, s_recv,
):
    (steps, width, cap, flight, n_seq, n_ctx, n_exp, n_tok, top, experts) = cfg
    n_y = n_ctx // 2
    slots = flight * SUBS
    rows = flight * cap
    length = n_tok * n_ctx * n_exp
    seq, ctx, exp = lax.axis_index("seq"), lax.axis_index("ctx"), lax.axis_index("exp")
    me = seq * n_exp + exp
    my_y, core = ctx // 2, ctx % 2

    def group(o):
        p = (me + o) % flight
        return p, (p // n_exp, ctx, p % n_exp)

    def y_peer(o):
        y = (my_y + o) % n_y
        return y, (seq, y * 2 + core, exp)

    partner = (seq, ctx + 1 - 2 * core, exp)

    barrier = pltpu.get_barrier_semaphore()
    for o in range(1, flight):
        pl.semaphore_signal(barrier, inc=1, device_id=group(o)[1], device_id_type=MESH)
    for o in range(1, n_ctx):
        pl.semaphore_signal(barrier, inc=1, device_id=(seq, (ctx + o) % n_ctx, exp), device_id_type=MESH)

    def local(c, which):
        cols = pl.ds(pl.multiple_of(c * width, width), width)
        src, dst, sem = (
            lambda: (tokens.at[0, :, cols], tok.at[c], tok_sem.at[c]),
            lambda: (router_weight.at[cols], rw.at[c], rw_sem.at[c]),
            lambda: (w_gate.at[0, cols], wg.at[c], wg_sem.at[c]),
            lambda: (w_up.at[0, cols], wu.at[c], wu_sem.at[c]),
            lambda: (w_down.at[0, :, cols], wd.at[c], wd_sem.at[c]),
            lambda: (outv.at[c], out.at[0, :, cols], out_sem.at[c]),
        )[which]()
        return pltpu.make_async_copy(src, dst, sem)

    for which in range(5):
        @pl.loop(0, steps)
        def _(c):
            local(c, which).start()

    rt = routes_t[...]
    slot_expert = lax.broadcasted_iota(jnp.int32, (slots, n_tok), 0)
    hit_t = jnp.zeros((slots, n_tok), f32)
    for k in range(top):
        hit_t = hit_t + (rt[k : k + 1, :] == slot_expert // SUBS).astype(f32)
    ti = lax.broadcasted_iota(jnp.int32, (n_tok, n_tok), 0)
    tj = lax.broadcasted_iota(jnp.int32, (n_tok, n_tok), 1)
    rank_t = dot(hit_t.astype(bf16), (ti < tj).astype(f32).astype(bf16))
    pick_t = jnp.where(rank_t == (slot_expert % SUBS).astype(f32), hit_t, 0.0)
    sel_s[...] = pick_t.astype(bf16)

    def dispatch(c, o):
        p, dev = group(o)
        return pltpu.make_async_remote_copy(
            src_ref=mout.at[c, p], dst_ref=minn.at[c, me], send_sem=d_send.at[c, o], recv_sem=d_recv.at[c, o],
            device_id=dev, device_id_type=MESH)

    def spread(c, o):
        _, dev = y_peer(o)
        return pltpu.make_async_remote_copy(
            src_ref=xs.at[c, ctx], dst_ref=xs.at[c, ctx], send_sem=y_send.at[c, o], recv_sem=y_recv.at[c, o],
            device_id=dev, device_id_type=MESH)

    def hand(c, o):
        y = (my_y + o) % n_y
        slot = y * 2 + core
        return pltpu.make_async_remote_copy(
            src_ref=xs.at[c, slot], dst_ref=xs.at[c, slot], send_sem=c_send.at[c, o], recv_sem=c_recv.at[c, o],
            device_id=partner, device_id_type=MESH)

    pl.semaphore_wait(barrier, flight - 1 + n_ctx - 1)

    @pl.loop(0, steps)
    def _(c):
        local(c, 0).wait()
        picked = dot(sel_s[...], tok[c]).reshape(flight, SUBS, width)
        mout[c] = pack(picked, cap).astype(bf16)
        minn[c, me] = mout[c, me]
        for o in range(1, flight):
            dispatch(c, o).start()

    acc_r = jnp.zeros((n_tok, experts), f32)

    def route_step(c, total):
        local(c, 1).wait()
        return total + dot(tok[c], rw[c])

    logits = lax.fori_loop(0, steps, route_step, acc_r)
    scores = jax.nn.sigmoid(logits)
    affinity = scores / jnp.sum(scores, axis=1, keepdims=True)
    rr = routes[0]
    lane = lax.broadcasted_iota(jnp.int32, (n_tok, experts), 1)
    hit = jnp.zeros((n_tok, experts), f32)
    for k in range(top):
        hit = hit + (rr[:, k : k + 1] == lane).astype(f32)
    gate = hit * scores / jnp.sum(hit * scores, axis=1, keepdims=True) * route_scale
    stat[ctx, 0:1] = jnp.sum(affinity, axis=0, keepdims=True)
    stat[ctx, 1:2] = jnp.sum(hit, axis=0, keepdims=True)

    def stat_ctx(o):
        return pltpu.make_async_remote_copy(
            src_ref=stat.at[ctx], dst_ref=stat.at[ctx], send_sem=s_send.at[o], recv_sem=s_recv.at[o],
            device_id=(seq, (ctx + o) % n_ctx, exp), device_id_type=MESH)

    def stat_exp(o):
        slot = n_ctx + exp
        return pltpu.make_async_remote_copy(
            src_ref=stat.at[slot], dst_ref=stat.at[slot], send_sem=s_send.at[n_ctx + o],
            recv_sem=s_recv.at[n_ctx + o], device_id=(seq, ctx, (exp + o) % n_exp), device_id_type=MESH)

    for o in range(1, n_ctx):
        stat_ctx(o).start()

    rank = dot((ti > tj).astype(f32).astype(bf16), hit.astype(bf16))
    ei = lax.broadcasted_iota(jnp.int32, (experts, slots), 0)
    ej = lax.broadcasted_iota(jnp.int32, (experts, slots), 1)
    widen = (ei == ej // SUBS).astype(f32).astype(bf16)
    place = (lax.broadcasted_iota(jnp.int32, (n_tok, slots), 1) % SUBS).astype(f32)
    here = dot(rank.astype(bf16), widen) == place
    high = gate.astype(bf16)
    low = (gate - high.astype(f32)).astype(bf16)
    gates[0] = jnp.where(here, dot(high, widen), 0.0).astype(bf16)
    gates[1] = jnp.where(here, dot(low, widen), 0.0).astype(bf16)

    ri = lax.broadcasted_iota(jnp.int32, (rows, slots), 0)
    rj = lax.broadcasted_iota(jnp.int32, (rows, slots), 1)
    squeeze = ((ri // cap == rj // SUBS) & (ri % cap == rj % SUBS)).astype(f32).astype(bf16)
    si = lax.broadcasted_iota(jnp.int32, (slots, rows), 0)
    sj = lax.broadcasted_iota(jnp.int32, (slots, rows), 1)
    expand = ((sj // cap == si // SUBS) & (sj % cap == si % SUBS)).astype(f32).astype(bf16)

    acc[...] = jnp.zeros_like(acc)

    @pl.loop(0, steps + 2)
    def _(i):
        @pl.when(i < steps)
        def _():
            c = i
            for o in range(1, flight):
                dispatch(c, o).wait_recv()
            loose = unpack(minn[c].astype(f32), cap).reshape(slots, width).astype(bf16)
            xs[c, ctx] = dot(squeeze, loose).astype(bf16)
            for o in range(1, n_y):
                spread(c, o).start()
            hand(c, 0).start()

        @pl.when((i >= 1) & (i < steps + 1))
        def _():
            c = i - 1
            for o in range(1, n_y):
                spread(c, n_y - o).wait_recv()
                hand(c, o).start()

        @pl.when(i >= 2)
        def _():
            c = i - 2
            for o in range(n_y):
                hand(c, o).wait_recv()
            x = jnp.concatenate([xs[c, j].astype(f32) for j in range(n_ctx)], axis=0).astype(bf16)
            local(c, 2).wait()
            local(c, 3).wait()
            acc[0] += dot(x, wg[c])
            acc[1] += dot(x, wu[c])

    gv = acc[0]
    hid[...] = (gv / (1.0 + jnp.exp(-gv)) * acc[1]).astype(bf16)

    for o in range(1, n_ctx):
        stat_ctx(o).wait_recv()
    ctx_total = stat[0]
    for j in range(1, n_ctx):
        ctx_total = ctx_total + stat[j]
    stat[n_ctx + exp] = ctx_total
    for o in range(1, n_exp):
        stat_exp(o).start()

    def pair(c):
        return pltpu.make_async_remote_copy(
            src_ref=ps.at[c], dst_ref=pr.at[c], send_sem=p_send.at[c], recv_sem=p_recv.at[c],
            device_id=partner, device_id_type=MESH)

    def back_y(c, o):
        y, dev = y_peer(o)
        return pltpu.make_async_remote_copy(
            src_ref=ys.at[c, o], dst_ref=yr.at[c, o], send_sem=v_send.at[c, o], recv_sem=v_recv.at[c, o],
            device_id=dev, device_id_type=MESH)

    def back(c, o):
        p, dev = group(o)
        return pltpu.make_async_remote_copy(
            src_ref=rout.at[c, p], dst_ref=rin.at[c, me], send_sem=r_send.at[c, o], recv_sem=r_recv.at[c, o],
            device_id=dev, device_id_type=MESH)

    @pl.loop(0, steps + 3)
    def _(i):
        @pl.when(i < steps)
        def _():
            c = i
            local(c, 4).wait()
            part = dot(hid[...], wd[c])
            for y in range(n_y):
                a = part[(2 * y) * rows : (2 * y + 1) * rows]
                b = part[(2 * y + 1) * rows : (2 * y + 2) * rows]
                ps[c, y] = jnp.where(core == 0, b, a).astype(bf16)
                keep[c, y] = jnp.where(core == 0, a, b).astype(bf16)
            pair(c).start()

        @pl.when((i >= 1) & (i < steps + 1))
        def _():
            c = i - 1
            pair(c).wait_recv()
            for o in range(n_y):
                y = (my_y + o) % n_y
                both = keep[c, y].astype(f32) + pr[c, y].astype(f32)
                if o == 0:
                    ykeep[c] = both
                else:
                    ys[c, o] = both.astype(bf16)
                    back_y(c, o).start()

        @pl.when((i >= 2) & (i < steps + 2))
        def _():
            c = i - 2
            total = ykeep[c]
            for o in range(1, n_y):
                back_y(c, o).wait_recv()
                total = total + yr[c, o].astype(f32)
            spaced = dot(expand, total.astype(bf16)).reshape(flight, SUBS, width)
            rout[c] = pack(spaced, cap).astype(bf16)
            rin[c, me] = rout[c, me]
            for o in range(1, flight):
                back(c, o).start()

        @pl.when(i >= 3)
        def _():
            c = i - 3
            for o in range(1, flight):
                back(c, o).wait_recv()
            got = unpack(rin[c].astype(f32), cap).reshape(slots, width).astype(bf16)
            outv[c] = (dot(gates[0], got) + dot(gates[1], got)).astype(bf16)
            local(c, 5).start()

    for o in range(1, n_exp):
        stat_exp(o).wait_recv()
    total = stat[n_ctx]
    for j in range(1, n_exp):
        total = total + stat[n_ctx + j]
    bal[...] = total[1:2] * (experts / (top * length)) * (total[0:1] / length) * experts

    for o in range(1, n_ctx):
        stat_ctx(o).wait_send()
    for o in range(1, n_exp):
        stat_exp(o).wait_send()

    @pl.loop(0, steps)
    def _(c):
        for o in range(1, flight):
            dispatch(c, o).wait_send()
            back(c, o).wait_send()
        for o in range(1, n_y):
            spread(c, o).wait_send()
            back_y(c, o).wait_send()
        for o in range(n_y):
            hand(c, o).wait_send()
        pair(c).wait_send()
        local(c, 5).wait()


def on_device(tokens, routing, router_weight, w_gate, w_up, w_down):
    n_seq, n_ctx, n_exp = (lax.axis_size(a) for a in ("seq", "ctx", "exp"))
    _, n_tok, features = tokens.shape
    top = routing.shape[2]
    experts = router_weight.shape[1]
    ff = w_gate.shape[2]
    flight = n_seq * n_exp
    mean_load = n_tok * top // experts
    cap = mean_load + mean_load // 4
    width = SUBS * LANES
    steps = features // width
    n_y = n_ctx // 2
    rows = flight * cap
    slots = flight * SUBS
    cfg = (steps, width, cap, flight, n_seq, n_ctx, n_exp, n_tok, top, experts)
    V = pltpu.VMEM
    dma = pltpu.SemaphoreType.DMA
    dense = cap * LANES
    scratch = [
        V((steps, n_tok, width), bf16), V((steps, width, experts), bf16), V((steps, width, ff), bf16),
        V((steps, width, ff), bf16), V((steps, ff, width), bf16), V((steps, n_tok, width), bf16),
        V((steps, flight, SUBS, dense), bf16), V((steps, flight, SUBS, dense), bf16),
        V((steps, n_ctx, rows, width), bf16), V((2, n_ctx * rows, ff), f32), V((slots, n_tok), bf16),
        V((2, n_tok, slots), bf16), V((n_ctx * rows, ff), bf16),
        V((steps, n_y, rows, width), bf16), V((steps, n_y, rows, width), bf16), V((steps, n_y, rows, width), bf16),
        V((steps, n_y, rows, width), bf16), V((steps, n_y, rows, width), bf16), V((steps, rows, width), f32),
        V((steps, flight, SUBS, dense), bf16), V((steps, flight, SUBS, dense), bf16),
        V((n_ctx + n_exp, 2, experts), f32),
    ]
    scratch += [dma((steps,)) for _ in range(6)]
    scratch += [dma((steps, flight)), dma((steps, flight)), dma((steps, n_y)), dma((steps, n_y)),
                dma((steps, n_y)), dma((steps, n_y)), dma((steps,)), dma((steps,)),
                dma((steps, n_y)), dma((steps, n_y)), dma((steps, flight)), dma((steps, flight)),
                dma((n_ctx + n_exp,)), dma((n_ctx + n_exp,))]
    hbm = pl.BlockSpec(memory_space=pl.ANY)
    vm = pl.BlockSpec(memory_space=pltpu.VMEM)
    return pl.pallas_call(
        functools.partial(kernel, cfg),
        out_shape=(jax.ShapeDtypeStruct(tokens.shape, bf16), jax.ShapeDtypeStruct((1, experts), f32)),
        in_specs=[hbm, vm, vm, hbm, hbm, hbm, hbm],
        out_specs=(hbm, vm),
        scratch_shapes=scratch,
        compiler_params=pltpu.CompilerParams(
            collective_id=0, has_side_effects=True, vmem_limit_bytes=60 * 1024 * 1024),
    )(tokens, routing, routing[0].T, router_weight, w_gate, w_up, w_down)


def solution(mesh):
    placed = (
        P("seq", ("ctx", "exp"), None),
        P("seq", ("ctx", "exp"), None),
        P(),
        P(("seq", "exp"), None, "ctx"),
        P(("seq", "exp"), None, "ctx"),
        P(("seq", "exp"), "ctx", None),
    )
    return jax.shard_map(
        on_device,
        mesh=mesh,
        in_specs=placed,
        out_specs=(P("seq", ("ctx", "exp"), None), P("seq", None)),
        check_vma=False,
    )
```

time: 198 us -> 70.7 us (0.36)
  Pallas kernels: 0 us -> 65 us
  blocking collectives: 64 us -> 0 us
  waiting for transfers between devices: 42.5 us -> 0 us
  local copies, waits for them, and re-layouts: 43.1 us -> 4.83 us
  matrix products: 17.8 us -> 0 us
  between operations: 14.2 us -> 0.65 us
  other arithmetic: 12.5 us -> 0 us
  starting transfers between devices: 3.81 us -> 0 us
    pallas_call x0 -> x1, Pallas kernels: none -> 65 us  [on_device(): pl.pallas_call(functools.partial(kernel, cfg), out_shape=(jax.ShapeDtypeS...]
    gather x14 -> x0, local copies, waits for them, and re-layouts: 33.7 us -> none  [the longest x8 23.7 us: on_device(): returned[row_index[:, column]]]
    psum x1 -> x0, blocking collectives: 33.1 us -> none  [on_device(): prob_sum, load_sum = lax.psum((prob_part, load_part), ('ctx', 'exp'))]
    all_to_all x1 -> x0, blocking collectives: 30.9 us -> none  [on_device(): lax.all_to_all(outgoing, ('seq', 'exp'), split_axis=0, concat_axis=0, til...]
    all_gather x1 -> x0, waiting for transfers between devices: 21.4 us -> none  [on_device(): lax.all_gather(lax.all_to_all(outgoing, ('seq', 'exp'), split_axis=0, con...]
    all_to_all x1 -> x0, waiting for transfers between devices: 21.1 us -> none  [on_device(): lax.all_to_all(summed, ('seq', 'exp'), split_axis=0, concat_axis=0, tiled...]
    dot_general x3 -> x0, matrix products: 17.8 us -> none  [the longest x2 15 us: project_rows(): jnp.dot(row_block.reshape(-1, layout[-1]), weight, preferred_element_type...]
    convert_element_type x2 -> x0, other arithmetic: 7.97 us -> none  [the longest x1 7.96 us: on_device(): return (combined.astype(jnp.bfloat16)[None], balance[None])]
  transfers between devices with their start and end apart: 3 -> 0, of which waited for: 2 -> 0; matrix products, arithmetic and copies ran while one was open for 7% -> 0% of each run, Pallas kernels for 0% -> 0%
where the time goes in v1:
time: 70.7 us; the launch traced here: 70.5 us
  Pallas kernels  65 us (92%)
  local copies, waits for them, and re-layouts  4.83 us (7%)
    pallas_call x1, Pallas kernels, on_device(): pl.pallas_call(functools.partial(kernel, cfg), out_shape=(jax.ShapeDtypeS...  65 us
    unnamed x5, local copies, waits for them, and re-layouts  4.83 us

profile of v1, /device:TPU:0, one launch (start us, length us, event | category | flops | bytes accessed | tf_op | source)
XLA Modules:
  0.0 70.5 jit_solution(15541698053622563750)
XLA Ops:
  0.6 1.4 %copy.8.routes = s32[1,128,8]{2,1,0:T(8,128)} copy(s32[1,128,8]{1,2,0:T(8,128)} %param.7) | data formatting | bytes 8192 | tf_op args[1]
  2.0 65.0 %shard_map.77 = (bf16[1,128,7168]{2,1,0:T(8,128)(2,1)}, f32[1,256]{1,0:T(1,128)}) custom-call(bf16[1,128,7168]{2,1,0:T(8,128)(2,1)} %tokens.1, s32[1,128,8]{2,1,0:T(8,128)} %copy.8.routes, s32[8,128]{1,0:T(8,128)} %bitcast.3, bf16[7168,256]{1,0:T(8,128)(2,1)} %router_weight.1, bf16[1,7168,512]{2,1,0:T(8,128)(2,1)} %w_gate.1, bf16[1,7168,512]{2,1,0:T(8,128)(2,1)} %w_up.1, ...), custom_call_target="tpu_custom_call" | custom-call | tf_op jit(solution)/shard_map/pallas_call | solution.py:364
  67.1 0.0 copy-start
  67.1 2.8 %copy.11 = bf16[1,128,7168]{2,1,0:T(8,128)(2,1)} copy(bf16[1,128,7168]{2,1,0:T(8,128)(2,1)} %get-tuple-element.4) | data formatting | bytes 3670016
  69.9 0.0 copy-done
  69.9 0.6 copy.12
Async XLA Ops:
  67.1 2.9 %copy-start = (f32[1,256]{1,0:T(1,128)S(1)}, f32[1,256]{1,0:T(1,128)}, u32[]{:S(2)}) copy-start(f32[1,256]{1,0:T(1,128)} %get-tuple-element.5) | copy-start | bytes 3076

commit v2 on v1

--- a/solution.py
+++ b/solution.py
@@ -46,10 +46,10 @@
 
 def kernel(
     cfg,
-    tokens, routes, routes_t, router_weight, w_gate, w_up, w_down,
+    tokens, routes_t, router_weight, w_gate, w_up, w_down,
     out, bal,
     tok, rw, wg, wu, wd, outv,
-    mout, minn, xs, acc, sel_s, gates, hid,
+    mout, minn, xs, acc, logits, sel_s, gates, hid,
     ps, pr, keep, ys, yr, ykeep, rout, rin, stat,
     tok_sem, rw_sem, wg_sem, wu_sem, wd_sem, out_sem,
     d_send, d_recv, y_send, y_recv, c_send, c_recv,
@@ -92,10 +92,9 @@
         )[which]()
         return pltpu.make_async_copy(src, dst, sem)
 
-    for which in range(5):
-        @pl.loop(0, steps)
-        def _(c):
-            local(c, which).start()
+    @pl.loop(0, steps)
+    def _(c):
+        local(c, 0).start()
 
     rt = routes_t[...]
     slot_expert = lax.broadcasted_iota(jnp.int32, (slots, n_tok), 0)
@@ -137,24 +136,12 @@
         minn[c, me] = mout[c, me]
         for o in range(1, flight):
             dispatch(c, o).start()
-
-    acc_r = jnp.zeros((n_tok, experts), f32)
-
-    def route_step(c, total):
-        local(c, 1).wait()
-        return total + dot(tok[c], rw[c])
-
-    logits = lax.fori_loop(0, steps, route_step, acc_r)
-    scores = jax.nn.sigmoid(logits)
-    affinity = scores / jnp.sum(scores, axis=1, keepdims=True)
-    rr = routes[0]
-    lane = lax.broadcasted_iota(jnp.int32, (n_tok, experts), 1)
-    hit = jnp.zeros((n_tok, experts), f32)
-    for k in range(top):
-        hit = hit + (rr[:, k : k + 1] == lane).astype(f32)
-    gate = hit * scores / jnp.sum(hit * scores, axis=1, keepdims=True) * route_scale
-    stat[ctx, 0:1] = jnp.sum(affinity, axis=0, keepdims=True)
-    stat[ctx, 1:2] = jnp.sum(hit, axis=0, keepdims=True)
+        for which in range(1, 4):
+            local(c, which).start()
+
+    @pl.loop(0, steps)
+    def _(c):
+        local(c, 4).start()
 
     def stat_ctx(o):
         return pltpu.make_async_remote_copy(
@@ -167,19 +154,40 @@
             src_ref=stat.at[slot], dst_ref=stat.at[slot], send_sem=s_send.at[n_ctx + o],
             recv_sem=s_recv.at[n_ctx + o], device_id=(seq, ctx, (exp + o) % n_exp), device_id_type=MESH)
 
-    for o in range(1, n_ctx):
-        stat_ctx(o).start()
-
-    rank = dot((ti > tj).astype(f32).astype(bf16), hit.astype(bf16))
-    ei = lax.broadcasted_iota(jnp.int32, (experts, slots), 0)
-    ej = lax.broadcasted_iota(jnp.int32, (experts, slots), 1)
-    widen = (ei == ej // SUBS).astype(f32).astype(bf16)
-    place = (lax.broadcasted_iota(jnp.int32, (n_tok, slots), 1) % SUBS).astype(f32)
-    here = dot(rank.astype(bf16), widen) == place
-    high = gate.astype(bf16)
-    low = (gate - high.astype(f32)).astype(bf16)
-    gates[0] = jnp.where(here, dot(high, widen), 0.0).astype(bf16)
-    gates[1] = jnp.where(here, dot(low, widen), 0.0).astype(bf16)
+    def weigh():
+        scores = jax.nn.sigmoid(logits[...])
+        affinity = scores / jnp.sum(scores, axis=1, keepdims=True)
+        spare = jnp.zeros((n_tok - top, n_tok), f32)
+        rr = jnp.concatenate([routes_t[...].astype(f32), spare], axis=0).T
+        lane = lax.broadcasted_iota(jnp.int32, (n_tok, experts), 1).astype(f32)
+        hit = jnp.zeros((n_tok, experts), f32)
+        for k in range(top):
+            hit = hit + (rr[:, k : k + 1] == lane).astype(f32)
+        gate = hit * scores / jnp.sum(hit * scores, axis=1, keepdims=True) * route_scale
+        stat[ctx, 0:1] = jnp.sum(affinity, axis=0, keepdims=True)
+        stat[ctx, 1:2] = jnp.sum(hit, axis=0, keepdims=True)
+        for o in range(1, n_ctx):
+            stat_ctx(o).start()
+        rank = dot((ti > tj).astype(f32).astype(bf16), hit.astype(bf16))
+        ei = lax.broadcasted_iota(jnp.int32, (experts, slots), 0)
+        ej = lax.broadcasted_iota(jnp.int32, (experts, slots), 1)
+        widen = (ei == ej // SUBS).astype(f32).astype(bf16)
+        place = (lax.broadcasted_iota(jnp.int32, (n_tok, slots), 1) % SUBS).astype(f32)
+        here = dot(rank.astype(bf16), widen) == place
+        high = gate.astype(bf16)
+        low = (gate - high.astype(f32)).astype(bf16)
+        gates[0] = jnp.where(here, dot(high, widen), 0.0).astype(bf16)
+        gates[1] = jnp.where(here, dot(low, widen), 0.0).astype(bf16)
+
+    def share():
+        for o in range(1, n_ctx):
+            stat_ctx(o).wait_recv()
+        ctx_total = stat[0]
+        for j in range(1, n_ctx):
+            ctx_total = ctx_total + stat[j]
+        stat[n_ctx + exp] = ctx_total
+        for o in range(1, n_exp):
+            stat_exp(o).start()
 
     ri = lax.broadcasted_iota(jnp.int32, (rows, slots), 0)
     rj = lax.broadcasted_iota(jnp.int32, (rows, slots), 1)
@@ -189,8 +197,11 @@
     expand = ((sj // cap == si // SUBS) & (sj % cap == si % SUBS)).astype(f32).astype(bf16)
 
     acc[...] = jnp.zeros_like(acc)
-
-    @pl.loop(0, steps + 2)
+    logits[...] = jnp.zeros_like(logits)
+    lag_c, lag_d = 2, 3
+    lag_f, lag_g, lag_h = 1, 4, 7
+
+    @pl.loop(0, steps + lag_d)
     def _(i):
         @pl.when(i < steps)
         def _():
@@ -202,17 +213,19 @@
             for o in range(1, n_y):
                 spread(c, o).start()
             hand(c, 0).start()
-
-        @pl.when((i >= 1) & (i < steps + 1))
-        def _():
-            c = i - 1
+            local(c, 1).wait()
+            logits[...] += dot(tok[c], rw[c])
+
+        @pl.when((i >= lag_c) & (i < steps + lag_c))
+        def _():
+            c = i - lag_c
             for o in range(1, n_y):
                 spread(c, n_y - o).wait_recv()
                 hand(c, o).start()
 
-        @pl.when(i >= 2)
-        def _():
-            c = i - 2
+        @pl.when(i >= lag_d)
+        def _():
+            c = i - lag_d
             for o in range(n_y):
                 hand(c, o).wait_recv()
             x = jnp.concatenate([xs[c, j].astype(f32) for j in range(n_ctx)], axis=0).astype(bf16)
@@ -224,15 +237,6 @@
     gv = acc[0]
     hid[...] = (gv / (1.0 + jnp.exp(-gv)) * acc[1]).astype(bf16)
 
-    for o in range(1, n_ctx):
-        stat_ctx(o).wait_recv()
-    ctx_total = stat[0]
-    for j in range(1, n_ctx):
-        ctx_total = ctx_total + stat[j]
-    stat[n_ctx + exp] = ctx_total
-    for o in range(1, n_exp):
-        stat_exp(o).start()
-
     def pair(c):
         return pltpu.make_async_remote_copy(
             src_ref=ps.at[c], dst_ref=pr.at[c], send_sem=p_send.at[c], recv_sem=p_recv.at[c],
@@ -250,7 +254,7 @@
             src_ref=rout.at[c, p], dst_ref=rin.at[c, me], send_sem=r_send.at[c, o], recv_sem=r_recv.at[c, o],
             device_id=dev, device_id_type=MESH)
 
-    @pl.loop(0, steps + 3)
+    @pl.loop(0, steps + lag_h)
     def _(i):
         @pl.when(i < steps)
         def _():
@@ -264,9 +268,9 @@
                 keep[c, y] = jnp.where(core == 0, a, b).astype(bf16)
             pair(c).start()
 
-        @pl.when((i >= 1) & (i < steps + 1))
-        def _():
-            c = i - 1
+        @pl.when((i >= lag_f) & (i < steps + lag_f))
+        def _():
+            c = i - lag_f
             pair(c).wait_recv()
             for o in range(n_y):
                 y = (my_y + o) % n_y
@@ -277,9 +281,17 @@
                     ys[c, o] = both.astype(bf16)
                     back_y(c, o).start()
 
-        @pl.when((i >= 2) & (i < steps + 2))
-        def _():
-            c = i - 2
+        @pl.when(i == lag_g - 1)
+        def _():
+            weigh()
+
+        @pl.when(i == lag_h - 1)
+        def _():
+            share()
+
+        @pl.when((i >= lag_g) & (i < steps + lag_g))
+        def _():
+            c = i - lag_g
             total = ykeep[c]
             for o in range(1, n_y):
                 back_y(c, o).wait_recv()
@@ -290,9 +302,9 @@
             for o in range(1, flight):
                 back(c, o).start()
 
-        @pl.when(i >= 3)
-        def _():
-            c = i - 3
+        @pl.when(i >= lag_h)
+        def _():
+            c = i - lag_h
             for o in range(1, flight):
                 back(c, o).wait_recv()
             got = unpack(rin[c].astype(f32), cap).reshape(slots, width).astype(bf16)
@@ -347,7 +359,8 @@
         V((steps, n_tok, width), bf16), V((steps, width, experts), bf16), V((steps, width, ff), bf16),
         V((steps, width, ff), bf16), V((steps, ff, width), bf16), V((steps, n_tok, width), bf16),
         V((steps, flight, SUBS, dense), bf16), V((steps, flight, SUBS, dense), bf16),
-        V((steps, n_ctx, rows, width), bf16), V((2, n_ctx * rows, ff), f32), V((slots, n_tok), bf16),
+        V((steps, n_ctx, rows, width), bf16), V((2, n_ctx * rows, ff), f32), V((n_tok, experts), f32),
+        V((slots, n_tok), bf16),
         V((2, n_tok, slots), bf16), V((n_ctx * rows, ff), bf16),
         V((steps, n_y, rows, width), bf16), V((steps, n_y, rows, width), bf16), V((steps, n_y, rows, width), bf16),
         V((steps, n_y, rows, width), bf16), V((steps, n_y, rows, width), bf16), V((steps, rows, width), f32),
@@ -364,12 +377,12 @@
     return pl.pallas_call(
         functools.partial(kernel, cfg),
         out_shape=(jax.ShapeDtypeStruct(tokens.shape, bf16), jax.ShapeDtypeStruct((1, experts), f32)),
-        in_specs=[hbm, vm, vm, hbm, hbm, hbm, hbm],
+        in_specs=[hbm, vm, hbm, hbm, hbm, hbm],
         out_specs=(hbm, vm),
         scratch_shapes=scratch,
         compiler_params=pltpu.CompilerParams(
             collective_id=0, has_side_effects=True, vmem_limit_bytes=60 * 1024 * 1024),
-    )(tokens, routing, routing[0].T, router_weight, w_gate, w_up, w_down)
+    )(tokens, routing[0].T, router_weight, w_gate, w_up, w_down)
 
 
 def solution(mesh):

time: 70.7 us -> 60 us (0.85)
  Pallas kernels: 65 us -> 55.8 us
  local copies, waits for them, and re-layouts: 4.83 us -> 3.41 us
    pallas_call x1, Pallas kernels: 65 us -> 55.8 us  [on_device(): pl.pallas_call(functools.partial(kernel, cfg), out_shape=(jax.ShapeDtypeS...]
    unnamed x5 -> x4, local copies, waits for them, and re-layouts: 4.83 us -> 3.41 us
where the time goes in v2:
time: 60 us; the launch traced here: 59.8 us
  Pallas kernels  55.8 us (93%)
  local copies, waits for them, and re-layouts  3.41 us (6%)
  between operations  0.65 us (1%)
    pallas_call x1, Pallas kernels, on_device(): pl.pallas_call(functools.partial(kernel, cfg), out_shape=(jax.ShapeDtypeS...  55.8 us
    unnamed x4, local copies, waits for them, and re-layouts  3.41 us

profile of v2, /device:TPU:0, one launch (start us, length us, event | category | flops | bytes accessed | tf_op | source)
XLA Modules:
  0.0 59.8 jit_solution(2924992384514066238)
XLA Ops:
  0.6 55.8 %shard_map.77 = (bf16[1,128,7168]{2,1,0:T(8,128)(2,1)}, f32[1,256]{1,0:T(1,128)}) custom-call(bf16[1,128,7168]{2,1,0:T(8,128)(2,1)} %tokens.1, s32[8,128]{1,0:T(8,128)} %bitcast.3, bf16[7168,256]{1,0:T(8,128)(2,1)} %router_weight.1, bf16[1,7168,512]{2,1,0:T(8,128)(2,1)} %w_gate.1, bf16[1,7168,512]{2,1,0:T(8,128)(2,1)} %w_up.1, bf16[1,512,7168]{2,1,0:T(8,128)(2,1)} %w_down.1), custom_call_target="tpu_custom_call" | custom-call | tf_op jit(solution)/shard_map/pallas_call | solution.py:377
  56.4 0.0 copy-start
  56.4 2.8 %copy.10 = bf16[1,128,7168]{2,1,0:T(8,128)(2,1)} copy(bf16[1,128,7168]{2,1,0:T(8,128)(2,1)} %get-tuple-element.4) | data formatting | bytes 3670016
  59.3 0.0 copy-done
  59.3 0.6 copy.11
Async XLA Ops:
  56.4 2.9 %copy-start = (f32[1,256]{1,0:T(1,128)S(1)}, f32[1,256]{1,0:T(1,128)}, u32[]{:S(2)}) copy-start(f32[1,256]{1,0:T(1,128)} %get-tuple-element.5) | copy-start | bytes 3076

commit v3 on v2

--- a/solution.py
+++ b/solution.py
@@ -198,8 +198,8 @@
 
     acc[...] = jnp.zeros_like(acc)
     logits[...] = jnp.zeros_like(logits)
-    lag_c, lag_d = 2, 3
-    lag_f, lag_g, lag_h = 1, 4, 7
+    lag_c, lag_d = 4, 5
+    lag_f, lag_g, lag_h = 1, 3, 6
 
     @pl.loop(0, steps + lag_d)
     def _(i):
@@ -216,6 +216,10 @@
             local(c, 1).wait()
             logits[...] += dot(tok[c], rw[c])
 
+        @pl.when(i == steps)
+        def _():
+            weigh()
+
         @pl.when((i >= lag_c) & (i < steps + lag_c))
         def _():
             c = i - lag_c
@@ -280,10 +284,6 @@
                 else:
                     ys[c, o] = both.astype(bf16)
                     back_y(c, o).start()
-
-        @pl.when(i == lag_g - 1)
-        def _():
-            weigh()
 
         @pl.when(i == lag_h - 1)
         def _():

time: 60 us -> 57.7 us (0.962)
  Pallas kernels: 55.8 us -> 53.5 us
    pallas_call x1, Pallas kernels: 55.8 us -> 53.5 us  [on_device(): pl.pallas_call(functools.partial(kernel, cfg), out_shape=(jax.ShapeDtypeS...]
where the time goes in v3:
time: 57.7 us; the launch traced here: 57.5 us
  Pallas kernels  53.5 us (93%)
  local copies, waits for them, and re-layouts  3.41 us (6%)
  between operations  0.65 us (1%)
    pallas_call x1, Pallas kernels, on_device(): pl.pallas_call(functools.partial(kernel, cfg), out_shape=(jax.ShapeDtypeS...  53.5 us
    unnamed x4, local copies, waits for them, and re-layouts  3.41 us

profile of v3, /device:TPU:0, one launch (start us, length us, event | category | flops | bytes accessed | tf_op | source)
XLA Modules:
  0.0 57.5 jit_solution(13029770847305882960)
XLA Ops:
  0.6 53.5 %shard_map.77 = (bf16[1,128,7168]{2,1,0:T(8,128)(2,1)}, f32[1,256]{1,0:T(1,128)}) custom-call(bf16[1,128,7168]{2,1,0:T(8,128)(2,1)} %tokens.1, s32[8,128]{1,0:T(8,128)} %bitcast.3, bf16[7168,256]{1,0:T(8,128)(2,1)} %router_weight.1, bf16[1,7168,512]{2,1,0:T(8,128)(2,1)} %w_gate.1, bf16[1,7168,512]{2,1,0:T(8,128)(2,1)} %w_up.1, bf16[1,512,7168]{2,1,0:T(8,128)(2,1)} %w_down.1), custom_call_target="tpu_custom_call" | custom-call | tf_op jit(solution)/shard_map/pallas_call | solution.py:377
  54.1 0.0 copy-start
  54.1 2.8 %copy.10 = bf16[1,128,7168]{2,1,0:T(8,128)(2,1)} copy(bf16[1,128,7168]{2,1,0:T(8,128)(2,1)} %get-tuple-element.4) | data formatting | bytes 3670016
  57.0 0.0 copy-done
  57.0 0.6 copy.11
Async XLA Ops:
  54.1 2.9 %copy-start = (f32[1,256]{1,0:T(1,128)S(1)}, f32[1,256]{1,0:T(1,128)}, u32[]{:S(2)}) copy-start(f32[1,256]{1,0:T(1,128)} %get-tuple-element.5) | copy-start | bytes 3076
